TPU v7x, 32 devices: a whole 2x2x4 slice. The times are simulated.
32 devices in a mesh: seq: 16 (over z, x, core), zero: 2 (over y).
Axes of the slice: x: 2, y: 2, z: 4, core: 2. Of those that a mesh axis runs over, the one named last changes fastest.
Arguments:
- tokens: bfloat16 [2, 2048, 2048], P('zero', 'seq'), may hold values from -6 to 6
- w_in: bfloat16 [2048, 2336], P('zero'), may hold values from -0.0625 to 0.0625
- a_log: float32 [32], replicated, may hold values from -8 to 0
- dt_bias: float32 [32], replicated, may hold values from -4.5 to -3.5
- d_skip: float32 [32], replicated, may hold values from 0.5 to 1.5
- grad_y: bfloat16 [2, 2048, 2048], P('zero', 'seq'), may hold values from -6 to 6
Outputs:
- y_out: bfloat16 [2, 2048, 2048], P('zero', 'seq')
- grad_tokens: bfloat16 [2, 2048, 2048], P('zero', 'seq')
- grad_w: float32 [2048, 2336], P(('seq', 'zero'))
All inputs are finite; a program needn't handle non-finite values.
Results may differ from a plain program's by a relative error of at most 0.013.
Values may be sent and summed in bfloat16 or wider, within the bound.
A program may use at most 128 MiB of HBM per device.

v0:
```python
import jax
import jax.numpy as jnp
from jax import lax
from jax.sharding import PartitionSpec as P


def carried_in(value, axis, join, neutral, backward):
    count, mine = (lax.axis_size(axis), lax.axis_index(axis))
    pieces = jax.tree.map(lambda part: lax.all_gather(part, axis), value)
    if backward:
        pieces = jax.tree.map(lambda part: part[::-1], pieces)
        mine = count - 1 - mine
    so_far = jax.tree.map(
        lambda part, zero: jnp.full_like(part, 0) + jnp.asarray(zero, part.dtype), value, neutral
    )

    def hop(position, so_far):
        longer = join(so_far, jax.tree.map(lambda part: part[position], pieces))
        return jax.tree.map(lambda new, old: jnp.where(position < mine, new, old), longer, so_far)

    return lax.fori_loop(0, count - 1, hop, so_far)


def block_ssd(xs, bm, cm, raw, start, a_log, dt_bias, d_skip):
    high = lax.Precision.HIGHEST
    dt = jax.nn.softplus(raw + dt_bias)
    loga = -jnp.exp(a_log) * dt
    cum = jnp.cumsum(loga, axis=0)
    count = xs.shape[0]
    later = (jnp.arange(count)[:, None] >= jnp.arange(count)[None, :])[:, :, None]
    spans = cum[:, None, :] - cum[None, :, :]
    decay = jnp.where(later, jnp.exp(jnp.where(later, spans, 0.0)), 0.0)
    scores = jnp.dot(cm, bm.T, precision=high)
    mixing = scores[:, :, None] * decay * dt[None, :, :]
    ssd = jnp.einsum("tsh,shp->thp", mixing, xs, precision=high)
    ssd = ssd + jnp.einsum("tn,th,hpn->thp", cm, jnp.exp(cum), start, precision=high)
    out = ssd + d_skip[None, :, None] * xs
    tail = jnp.exp(cum[-1:] - cum) * dt
    state = jnp.exp(cum[-1])[:, None, None] * start + jnp.einsum(
        "sh,sn,shp->hpn", tail, bm, xs, precision=high
    )
    return (out, state)


def carry_forward(earlier, later):
    return (earlier[0] + later[0], jnp.exp(later[0])[:, None, None] * earlier[1] + later[1])


def carry_backward(earlier, later):
    return (earlier[0] + later[0], later[1] + jnp.exp(later[0])[:, None, None] * earlier[1])


def rounded(values):
    return lax.optimization_barrier(values.astype(jnp.bfloat16)).astype(jnp.float32)


def per_device(tokens, w_in, a_log, dt_bias, d_skip, grad_y):
    high = lax.Precision.HIGHEST
    count = tokens.shape[1]
    width = tokens.shape[2]
    inner = grad_y.shape[2]
    heads = a_log.shape[0]
    head_width = inner // heads
    state_width = (w_in.shape[1] - inner - heads) // 2
    columns_all = w_in.shape[1]
    rows = tokens.reshape(count, width)
    full_w = lax.all_gather(w_in, "zero", axis=0, tiled=True)
    proj = jnp.dot(rows, full_w, preferred_element_type=jnp.float32)
    xs = rounded(proj[:, :inner]).reshape(count, heads, head_width)
    bm = rounded(proj[:, inner : inner + state_width])
    cm = rounded(proj[:, inner + state_width : inner + 2 * state_width])
    raw = proj[:, inner + 2 * state_width :]
    dt = jax.nn.softplus(raw + dt_bias)
    cum = jnp.cumsum(-jnp.exp(a_log) * dt, axis=0)
    total = cum[-1]
    empty_state = jnp.zeros((heads, head_width, state_width), jnp.float32)
    empty_total = jnp.zeros((heads,), jnp.float32)
    local_out, local_state = block_ssd(xs, bm, cm, raw, empty_state, a_log, dt_bias, d_skip)
    prior = carried_in(
        (total, local_state), "seq", carry_forward, (empty_total, empty_state), False
    )
    start_state = prior[1]
    growth = jnp.exp(cum)
    outputs = local_out + jnp.einsum("tn,th,hpn->thp", cm, growth, start_state, precision=high)
    y_out = outputs.reshape(1, count, inner).astype(jnp.bfloat16)
    cotangent = grad_y.reshape(count, heads, head_width).astype(jnp.float32)
    back_local = jnp.einsum("tn,th,thp->hpn", cm, growth, cotangent, precision=high)
    after = carried_in((total, back_local), "seq", carry_backward, (empty_total, empty_state), True)
    end_adjoint = after[1]

    def local_layer(xin, bin_, cin, rin, sin):
        return block_ssd(xin, bin_, cin, rin, sin, a_log, dt_bias, d_skip)

    unused, pullback = jax.vjp(local_layer, xs, bm, cm, raw, start_state)
    grad_x, grad_b, grad_c, grad_raw, unused_state = pullback((cotangent, end_adjoint))
    gproj = jnp.concatenate(
        [grad_x.reshape(count, inner), grad_b, grad_c, grad_raw], axis=1
    ).astype(jnp.bfloat16)
    grad_rows = lax.dot_general(
        gproj, full_w, (((1,), (1,)), ((), ())), preferred_element_type=jnp.float32
    )
    grad_tokens = grad_rows.astype(jnp.bfloat16).reshape(1, count, width)
    seq_count = lax.axis_size("seq")
    zero_count = lax.axis_size("zero")
    piece = width // (seq_count * zero_count)
    owned = width // zero_count
    permuted = (
        rows.reshape(count, seq_count, zero_count, piece)
        .transpose(0, 2, 1, 3)
        .reshape(count, width)
    )
    received = lax.all_to_all(permuted, "zero", split_axis=1, concat_axis=0, tiled=True)
    pieces = lax.all_gather(gproj, "zero", axis=0, tiled=True)
    length = pieces.shape[0]
    shards = length // count
    parts = jnp.einsum(
        "ktr,kte->kre",
        received.reshape(shards, count, owned),
        pieces.reshape(shards, count, columns_all),
        preferred_element_type=jnp.float32,
    )
    zero_rows = jnp.sum(rounded(parts), axis=0)
    grad_w = lax.psum_scatter(zero_rows, "seq", scatter_dimension=0, tiled=True)
    return (y_out, grad_tokens, grad_w)


def solution(mesh):
    placed = (P("zero", "seq", None), P("zero", None), P(), P(), P(), P("zero", "seq", None))
    return jax.shard_map(
        per_device,
        mesh=mesh,
        in_specs=placed,
        out_specs=(P("zero", "seq", None), P("zero", "seq", None), P(("seq", "zero"), None)),
        check_vma=False,
    )
```

profile of v0, /device:TPU:0, one launch (start us, length us, event | category | flops | bytes accessed | tf_op | source)
XLA Modules:
  0.0 654.3 jit_solution(4928769661147055965)
XLA Ops:
  8.5 123.2 %all-gather.8.cloned.1.call-done = bf16[2048,2336]{0,1:T(8,128)(2,1)} async-done(((bf16[1024,2336]{0,1:T(8,128)(2,1)}), bf16[2048,2336]{0,1:T(8,128)(2,1)}) %all-gather.8.cloned.1.call-update) | async-done | bytes 9568272 | tf_op jit(solution)/shard_map/all_gather | solution.py:67
  131.7 5.3 fusion.75
  137.5 1.6 fusion.29
  139.3 21.8 %all-gather.2 = f32[16,1,32]{2,1,0:T(1,128)S(1)} all-gather(f32[1,1,32]{2,1,0:T(1,128)S(1)} %get-tuple-element.277), channel_id=1, replica_groups=mesh['seq'=16,'zero'=2] {'seq'}, dimensions={0}, use_global_device_ids=true | all-gather | bytes 2176 | tf_op jit(solution)/shard_map/all_gather | solution.py:9
  161.1 104.6 %all-gather.14.cloned.1.call-done = f32[512,64,128]{2,1,0:T(8,128)} async-done(((f32[32,64,128]{2,1,0:T(8,128)}), f32[512,64,128]{2,1,0:T(8,128)}) %all-gather.14.cloned.1.call-update) | async-done | bytes 16777232 | tf_op jit(solution)/shard_map/all_gather | solution.py:9
  265.7 11.8 %rev.6 = f32[16,32,64,128]{3,2,1,0:T(8,128)} reverse(f32[16,32,64,128]{3,2,1,0:T(8,128)} %bitcast.124), dimensions={0} | reverse | bytes 33554432 | tf_op jit(solution)/shard_map/rev | solution.py:11
  277.5 22.5 %while.29 = (s32[]{:T(128)}, f32[32,64,128]{2,1,0:T(8,128)S(1)}, s32[]{:T(128)}, f32[16,32,64,128]{3,2,1,0:T(8,128)}, f32[16,32]{1,0:T(8,128)S(1)}, /*index=5*/s32[]{:T(128)}, s32[]{:T(128)}) while((s32[]{:T(128)}, f32[32,64,128]{2,1,0:T(8,128)S(1)}, s32[]{:T(128)}, f32[16,32,64,128]{3,2,1,0:T(8,128)}, f32[16,32]{1,0:T(8,128)S(1)}, ...), condition=%wide.region_4.5_spmd.clone, body=%wide.region_3.4_spmd.clone.sunk | while | flops 1048580 | bytes 3146217 | solution.py:21
  277.5 1.5 fusion.97
  279.0 1.5 fusion.97
  280.5 1.5 fusion.97
  282.0 1.5 fusion.97
  283.5 1.5 fusion.97
  285.1 1.5 fusion.97
  288.1 1.5 fusion.97
  300.1 1.7 fusion.36
  302.4 1.7 convolution_add_fusion
  305.3 3.7 fusion.23
  309.0 2.1 copy.140
  311.1 1.8 fusion.30
  313.0 3.5 fusion.34
  321.1 107.8 %all-gather.12.cloned.1.call-done = f32[512,64,128]{2,1,0:T(8,128)} async-done(((f32[32,64,128]{2,1,0:T(8,128)}), f32[512,64,128]{2,1,0:T(8,128)}) %all-gather.12.cloned.1.call-update) | async-done | bytes 16777232 | tf_op jit(solution)/shard_map/all_gather | solution.py:9
  428.9 40.6 %while.28 = (s32[]{:T(128)}, f32[32,64,128]{2,1,0:T(8,128)S(1)}, s32[]{:T(128)}, f32[16,32]{1,0:T(8,128)}, f32[16,32,64,128]{3,2,1,0:T(8,128)}, /*index=5*/s32[]{:T(128)}, s32[]{:T(128)}) while((s32[]{:T(128)}, f32[32,64,128]{2,1,0:T(8,128)S(1)}, s32[]{:T(128)}, f32[16,32]{1,0:T(8,128)}, f32[16,32,64,128]{3,2,1,0:T(8,128)}, ...), condition=%wide.region_2.3_spmd.clone, body=%wide.region_1.2_spmd.clone.sunk | while | flops 1048580 | bytes 3146217 | solution.py:21
  469.5 1.8 convolution_bitcast_fusion.1
  478.1 1.9 pad_maximum_fusion
  480.7 15.3 %all_to_all.16 = bf16[128,2,1024]{2,0,1:T(8,128)(2,1)S(1)} all-to-all(bf16[128,2,1024]{2,0,1:T(8,128)(2,1)S(1)} %copy.145), channel_id=1, replica_groups=mesh['seq'=16,'zero'=2] {'zero'}, dimensions={1} | all-to-all | bytes 1048576 | tf_op jit(solution)/shard_map/all_to_all | solution.py:112
  496.0 9.4 %all-gather.10.cloned.1.call-done = bf16[256,2336]{1,0:T(8,128)(2,1)} async-done(((bf16[128,2336]{1,0:T(8,128)(2,1)}), bf16[256,2336]{1,0:T(8,128)(2,1)}) %all-gather.10.cloned.1.call-update) | async-done | bytes 1196048 | tf_op jit(solution)/shard_map/all_gather | solution.py:113
  505.4 6.5 convert_bitcast_fusion
  511.9 11.3 %convert_reduce_fusion = f32[1024,2336]{0,1:T(8,128)} fusion(bf16[2,1024,2336]{1,2,0:T(8,128)(2,1)} %convert_bitcast_fusion), kind=kLoop, calls=%fused_computation.6 | loop fusion | flops 7176192 | bytes 19136512 | tf_op jit(solution)/shard_map/reduce_sum | solution.py:122
  523.2 10.5 %copy.171 = f32[1024,2336]{1,0:T(8,128)} copy(f32[1024,2336]{0,1:T(8,128)} %convert_reduce_fusion) | data formatting | bytes 19136512
  534.5 2.4 fusion.11
  538.7 7.2 %fusion.2 = bf16[1,128,2048]{2,1,0:T(8,128)(2,1)} fusion(bf16[2048,2336]{0,1:T(8,128)(2,1)} %all-gather.8.cloned.1.call-done, bf16[128,32]{1,0:T(8,128)(2,1)S(1)} %fusion.62, bf16[128,128]{1,0:T(8,128)(2,1)S(1)} %copy.142, bf16[128,128]{1,0:T(8,128)(2,1)S(1)} %copy-done.4, bf16[128,2048]{1,0:T(8,128)(2,1)S(1)} %copy-done.2), kind=kOutput, calls=%fused_computation.9 | convolution fusion | flops 1227390976 | bytes 10690560 | tf_op jit(solution)/shard_map/dot_general | solution.py:99
  545.9 101.9 %reduce-scatter.4.cloned.1.call-done = f32[64,2336]{1,0:T(8,128)} async-done(((f32[1024,2336]{1,0:T(8,128)}), f32[64,2336]{1,0:T(8,128)}) %reduce-scatter.4.cloned.1.call-update) | async-done | bytes 598032
  (140 shorter events, 70.5 us)
Async XLA Ops:
  7.2 1.0 copy-start.3
  7.2 1.3 copy-start.17
  7.2 124.6 %copy-start = (bf16[1,128,2048]{2,1,0:T(8,128)(2,1)S(1)}, bf16[1,128,2048]{2,1,0:T(8,128)(2,1)}, u32[]{:S(2)}) copy-start(bf16[1,128,2048]{2,1,0:T(8,128)(2,1)} %param.10) | copy-start | bytes 1572868
  7.2 124.5 %all-gather.8.cloned.1.call-start = ((), (), s32[]{:S(2)}) async-start(), calls=%async_computation.2 | async-start | bytes 14352384 | tf_op jit(solution)/shard_map/all_gather | solution.py:67
  7.9 257.8 %all-gather.14.cloned.1.call-start = ((), (), s32[]{:S(2)}) async-start(), calls=%async_computation.5 | async-start | bytes 17825792 | tf_op jit(solution)/shard_map/all_gather | solution.py:9
  8.5 128.6 %copy-start.15 = (f32[32]{0:T(128)}, f32[32]{0:T(128)S(1)}, u32[]{:S(2)}) copy-start(f32[32]{0:T(128)S(1)} %exponential_negate_fusion) | copy-start | bytes 388
  8.5 128.6 %copy-start.13 = (f32[32]{0:T(128)S(1)}, f32[32]{0:T(128)}, u32[]{:S(2)}) copy-start(f32[32]{0:T(128)} %param.13) | copy-start | bytes 388
  139.1 289.8 %all-gather.12.cloned.1.call-start = ((), (), s32[]{:S(2)}) async-start(), calls=%async_computation.4 | async-start | bytes 17825792 | tf_op jit(solution)/shard_map/all_gather | solution.py:9
  139.3 162.6 %copy-start.14 = (f32[32]{0:T(128)}, f32[32]{0:T(128)S(1)}, u32[]{:S(2)}) copy-start(f32[32]{0:T(128)S(1)} %get-tuple-element.276) | copy-start | bytes 388
  161.1 116.4 %copy-start.6 = (f32[16,1,32]{2,1,0:T(1,128)}, f32[16,1,32]{2,1,0:T(1,128)S(1)}, u32[]{:S(2)}) copy-start(f32[16,1,32]{2,1,0:T(1,128)S(1)} %all-gather.2) | copy-start | bytes 6148
  304.1 201.2 %all-gather.10.cloned.1.call-start = ((), (), s32[]{:S(2)}) async-start(), calls=%async_computation.3 | async-start | bytes 1867776 | tf_op jit(solution)/shard_map/all_gather | solution.py:113
  304.4 8.6 %copy-start.11 = (pred[128,128]{1,0:T(8,128)(4,1)}, pred[128,128]{1,0:T(8,128)(4,1)S(1)}, u32[]{:S(2)}) copy-start(pred[128,128]{1,0:T(8,128)(4,1)S(1)} %iota_compare_fusion) | copy-start | bytes 49156
  304.5 8.5 %copy-start.7 = (f32[128,32]{0,1:T(8,128)}, f32[128,32]{0,1:T(8,128)S(1)}, u32[]{:S(2)}) copy-start(f32[128,32]{0,1:T(8,128)S(1)} %copy.126) | copy-start | bytes 49156
  305.3 7.6 %copy-start.9 = (f32[128,32]{0,1:T(8,128)}, f32[128,32]{0,1:T(8,128)S(1)}, u32[]{:S(2)}) copy-start(f32[128,32]{0,1:T(8,128)S(1)} %copy.128) | copy-start | bytes 49156
  473.4 6.8 %copy-start.1 = (bf16[1,128,2048]{2,1,0:T(8,128)(2,1)S(1)}, bf16[1,128,2048]{2,1,0:T(8,128)(2,1)}, u32[]{:S(2)}) copy-start(bf16[1,128,2048]{2,1,0:T(8,128)(2,1)} %param.10) | copy-start | bytes 1572868
  480.1 167.7 %reduce-scatter.4.cloned.1.call-start = ((), (), s32[]{:S(2)}) async-start(), calls=%async_computation.6 | async-start | bytes 10584064
  533.7 0.8 copy-start.5
  533.7 0.8 copy-start.8
  533.7 0.8 copy-start.10
  533.7 0.8 copy-start.12
  534.5 2.4 copy-start.16
  537.0 1.7 copy-start.2
  537.0 1.7 copy-start.4
Sparse Core Ops, SparseCore 0:
  9.6 122.1 all-gather.7
  139.2 126.4 all-gather.13
  304.2 124.5 all-gather.11
  480.2 25.1 all-gather.9
  533.8 113.8 reduce-scatter.3
where the time goes:
time: 657 us; the launch traced here: 654 us
  waiting for transfers between devices  448 us (68%)
  other arithmetic  62.3 us (9%)
  local copies, waits for them, and re-layouts  51.7 us (8%)
  matrix products  40.3 us (6%)
  blocking collectives  37.1 us (6%)
  between operations  14.1 us (2%)
    all_gather x2, waiting for transfers between devices, carried_in(): pieces = jax.tree.map(lambda part: lax.all_gather(part, axis), value)  212 us
    all_gather x1, waiting for transfers between devices, per_device(): full_w = lax.all_gather(w_in, 'zero', axis=0, tiled=True)  123 us
    unnamed x6, waiting for transfers between devices  103 us
    select_n x30, other arithmetic, hop(): jnp.where(position < mine, new, old)  43.8 us
    all_gather x1, blocking collectives, carried_in(): pieces = jax.tree.map(lambda part: lax.all_gather(part, axis), value)  21.8 us
    exp x15, local copies, waits for them, and re-layouts, carry_forward(): jnp.exp(later[0])[:, None, None] * earlier[1] + later[1]  18.4 us
    all_to_all x1, blocking collectives, per_device(): lax.all_to_all(permuted, 'zero', split_axis=1, concat_axis=0, tiled=True)  15.3 us
    unnamed x41, local copies, waits for them, and re-layouts  13.2 us
  transfers between devices with their start and end apart: 5, of which 5 were waited for; matrix products, arithmetic and copies ran while one was open for 4% of the time, Pallas kernels for 0%

commit v1 on v0

v1 whole, which is shorter than its diff:
```python
import jax
import jax.numpy as jnp
from jax import lax
from jax.sharding import PartitionSpec as P

BF = jnp.bfloat16
F32 = jnp.float32


def shift(value, axis, step):
    count = lax.axis_size(axis)
    return lax.ppermute(value, axis, [(i, (i + step) % count) for i in range(count)])


def flip(value, axis, bit):
    count = lax.axis_size(axis)
    return lax.ppermute(value, axis, [(i, i ^ bit) for i in range(count)])


def dot(a, b, dims):
    return lax.dot_general(a, b, (dims, ((), ())), preferred_element_type=F32)


def bdot(a, b, spec):
    return jnp.einsum(spec, a, b, preferred_element_type=F32)


def scan_states(states, totals):
    count = states.shape[0]
    fwd, bwd = states[:, :, 0].astype(F32), states[:, :, 1].astype(F32)
    run, ahead = [jnp.zeros_like(fwd[0])], [jnp.zeros_like(bwd[0])]
    for k in range(count - 1):
        run.append(jnp.exp(totals[k])[:, None, None] * run[-1] + fwd[k])
    for k in range(count - 1, 0, -1):
        ahead.append(jnp.exp(totals[k])[:, None, None] * ahead[-1] + bwd[k])
    return jnp.stack(
        [jnp.stack(run).astype(BF), jnp.stack(ahead[::-1]).astype(BF)], axis=2
    )


def ssd_block(proj, gy, a_log, dt_bias, d_skip):
    count, inner = gy.shape
    heads = a_log.shape[0]
    width = inner // heads
    size = (proj.shape[1] - inner - heads) // 2
    xs = proj[:, :inner].astype(BF)
    bm = proj[:, inner : inner + size].astype(BF)
    cm = proj[:, inner + size : inner + 2 * size].astype(BF)
    raw = proj[:, inner + 2 * size :] + dt_bias
    dt = jax.nn.softplus(raw)
    rate = -jnp.exp(a_log)
    lower = jnp.arange(count)[:, None] >= jnp.arange(count)[None, :]
    cum = jnp.dot(lower.astype(F32), rate * dt, precision=lax.Precision.HIGHEST)
    total = cum[-1]
    growth = jnp.exp(cum)
    fade = jnp.exp(total - cum)
    x3 = xs.reshape(count, heads, width).astype(F32)
    g3 = gy.reshape(count, heads, width).astype(F32)
    xd = (x3 * dt[:, :, None]).astype(BF)
    grown = (g3 * growth[:, :, None]).astype(BF).reshape(count, inner)
    faded = (xd.astype(F32) * fade[:, :, None]).astype(BF).reshape(count, inner)
    local_f = dot(faded, bm, ((0,), (0,)))
    local_g = dot(grown, cm, ((0,), (0,)))
    shape = (heads, width, size)
    pair = jnp.stack([local_f.reshape(shape), local_g.reshape(shape)], axis=1).astype(BF)

    seq = lax.axis_size("seq")
    mine = lax.axis_index("seq")
    share = heads // seq
    totals = lax.all_gather(total, "seq")
    got = lax.all_to_all(
        pair.reshape(seq, share, 2, width, size), "seq", split_axis=0, concat_axis=0, tiled=True
    )
    own = lax.dynamic_slice_in_dim(totals, mine * share, share, axis=1)
    back = lax.all_to_all(scan_states(got, own), "seq", split_axis=0, concat_axis=0, tiled=True)
    start = back[:, :, 0].reshape(inner, size)
    end = back[:, :, 1].reshape(inner, size)

    spans = cum.T[:, :, None] - cum.T[:, None, :]
    decay = jnp.where(lower[None], jnp.exp(jnp.where(lower[None], spans, 0.0)), 0.0)
    scores = dot(cm, bm, ((1,), (1,)))
    mixing = (scores[None] * decay).astype(BF)
    gb3 = gy.reshape(count, heads, width)
    y_in = bdot(mixing, xd, "hts,shp->thp")
    back_in = bdot(mixing, gb3, "hts,thp->shp")
    cross = bdot(gb3, xd, "thp,shp->hts")
    mixed = jnp.sum(cross * decay, axis=0).astype(BF)

    y3 = y_in + dot(cm, start, ((1,), (1,))).reshape(x3.shape) * growth[:, :, None]
    h3 = back_in + dot(bm, end, ((1,), (1,))).reshape(x3.shape) * fade[:, :, None]
    out = y3 + d_skip[:, None] * x3
    grad_x = h3 * dt[:, :, None] + d_skip[:, None] * g3
    grad_c = dot(mixed, bm, ((1,), (0,))) + dot(grown, start, ((1,), (0,)))
    grad_b = dot(mixed, cm, ((0,), (0,))) + dot(faded, end, ((1,), (0,)))
    row = jnp.sum(g3 * y3, axis=2)
    column = jnp.sum(xd.astype(F32) * h3, axis=2)
    grad_dt = jnp.sum(x3 * h3, axis=2)
    joint = jnp.sum((start.astype(F32) * end.astype(F32)).reshape(heads, -1), axis=1)
    tail = jnp.sum(
        xd.astype(F32) * dot(bm, end, ((1,), (1,))).reshape(x3.shape) * fade[:, :, None], axis=(0, 2)
    )
    last = tail + jnp.exp(total) * joint
    grad_log = jnp.dot(
        lower.astype(F32).T, row - column, precision=lax.Precision.HIGHEST
    ) + last
    grad_raw = (grad_dt + grad_log * rate) * jax.nn.sigmoid(raw)
    gproj = jnp.concatenate(
        [grad_x.reshape(count, inner), grad_b, grad_c, grad_raw], axis=1
    ).astype(BF)
    return out.reshape(count, inner).astype(BF), gproj


def halving(piece_sum, bits, names):
    mine = lax.axis_index("seq")
    for name in bits:
        at = names.index(name)
        bit = (mine // name) % 2
        away = lax.dynamic_index_in_dim(piece_sum, 1 - bit, at, keepdims=False)
        keep = lax.dynamic_index_in_dim(piece_sum, bit, at, keepdims=False)
        piece_sum = keep + flip(away.astype(BF), "seq", name).astype(F32)
        names = names[:at] + names[at + 1 :]
    return piece_sum


def per_device(tokens, w_in, a_log, dt_bias, d_skip, grad_y):
    count, width = tokens.shape[1:]
    inner = grad_y.shape[2]
    heads = a_log.shape[0]
    columns = w_in.shape[1]
    exact = columns - heads
    zero = lax.axis_size("zero")
    seq = lax.axis_size("seq")
    here = lax.axis_index("zero")
    place = lax.axis_index("seq")
    owned = width // zero
    rows = tokens.reshape(count, width)

    def columns_of(z):
        return lax.dynamic_slice_in_dim(rows, z * owned, owned, axis=1)

    guests = [shift(columns_of((here + s) % zero), "zero", s) for s in range(1, zero)]
    proj = jnp.dot(columns_of(here), w_in, preferred_element_type=F32)
    for s, guest in zip(range(1, zero), guests):
        part = jnp.dot(guest, w_in, preferred_element_type=F32)
        wide = shift(part[:, :exact].astype(BF), "zero", zero - s)
        narrow = shift(part[:, exact:], "zero", zero - s)
        proj = proj + jnp.concatenate([wide.astype(F32), narrow], axis=1)

    piece = width // (seq * zero)
    cut = rows.reshape(count, seq, zero, piece)

    def pieces_of(z):
        return lax.dynamic_index_in_dim(cut, z, 2, keepdims=False).reshape(count, seq * piece)

    theirs = [shift(pieces_of((here + s) % zero), "zero", s) for s in range(1, zero)]

    y_out, gproj = ssd_block(proj, grad_y.reshape(count, inner), a_log, dt_bias, d_skip)

    others = [shift(gproj, "zero", s) for s in range(1, zero)]
    mine = dot(gproj, w_in, ((1,), (1,))).astype(BF)
    grads = jnp.zeros((count, zero, owned), BF)
    grads = lax.dynamic_update_slice_in_dim(grads, mine[:, None], here, axis=1)
    for s, other in zip(range(1, zero), others):
        made = shift(dot(other, w_in, ((1,), (1,))).astype(BF), "zero", zero - s)
        grads = lax.dynamic_update_slice_in_dim(grads, made[:, None], (here + s) % zero, axis=1)
    grad_tokens = grads.reshape(1, count, width)

    left = jnp.concatenate([pieces_of(here)] + theirs, axis=0)
    right = jnp.concatenate([gproj] + others, axis=0)
    levels = seq.bit_length() - 1
    names = [1 << b for b in reversed(range(levels))]
    core = place % 2
    left = left.reshape(left.shape[0], seq // 2, 2, piece)

    def partial(core_of, span):
        chosen = lax.dynamic_index_in_dim(left, core_of, 2, keepdims=False)
        chosen = chosen.reshape(left.shape[0], seq // 2 * piece)
        return dot(chosen, right[:, span], ((0,), (0,)))

    done = []
    half = columns // 2 // 128 * 128
    rest = names[:-1]
    for span, order in (
        (slice(0, half), rest[::-1]),
        (slice(half, columns), rest[:-1][::-1] + rest[-1:]),
    ):
        swapped = flip(partial(1 - core, span).astype(BF), "seq", 1)
        summed = partial(core, span) + swapped.astype(F32)
        summed = summed.reshape([2] * (levels - 1) + [piece, summed.shape[1]])
        done.append(halving(summed, order, rest))
    grad_w = jnp.concatenate(done, axis=1)
    return (y_out.reshape(1, count, inner), grad_tokens, grad_w)


def solution(mesh):
    placed = (P("zero", "seq", None), P("zero", None), P(), P(), P(), P("zero", "seq", None))
    return jax.shard_map(
        per_device,
        mesh=mesh,
        in_specs=placed,
        out_specs=(P("zero", "seq", None), P("zero", "seq", None), P(("seq", "zero"), None)),
        check_vma=False,
    )
```

time: 657 us -> 239 us (0.36)
  waiting for transfers between devices: 448 us -> 95.6 us
  other arithmetic: 62.3 us -> 8.32 us
  starting transfers between devices: 0.38 us -> 29.5 us
  between operations: 14.1 us -> 1.11 us
  local copies, waits for them, and re-layouts: 51.7 us -> 39.1 us
  matrix products: 40.3 us -> 28.9 us
    all_gather x4 -> x0, waiting for transfers between devices: 345 us -> none  [the longest x2 212 us: carried_in(): pieces = jax.tree.map(lambda part: lax.all_gather(part, axis), value)]
    unnamed x6 -> x0, waiting for transfers between devices: 103 us -> none
    ppermute x0 -> x14, waiting for transfers between devices: none -> 74 us  [the longest x6 38 us: shift(): lax.ppermute(value, axis, [(i, (i + step) % count) for i in range(count)])]
    select_n x30 -> x1, other arithmetic: 43.8 us -> 0.09 us  [ssd_block(): dt = jax.nn.softplus(raw)]
    all_to_all x0 -> x2, waiting for transfers between devices: none -> 21.6 us  [the longest x1 21.6 us: ssd_block(): lax.all_to_all(scan_states(got, own), 'seq', split_axis=0, concat_axis=0,...]
    dynamic_update_slice x0 -> x2, local copies, waits for them, and re-layouts: none -> 18.8 us  [the longest x1 9.38 us: per_device(): grads = lax.dynamic_update_slice_in_dim(grads, mine[:, None], here, axis=1)]
    exp x32 -> x0, local copies, waits for them, and re-layouts: 18.6 us -> none  [the longest x15 18.4 us: carry_forward(): jnp.exp(later[0])[:, None, None] * earlier[1] + later[1]]
    ppermute x0 -> x14, starting transfers between devices: none -> 17.8 us  [the longest x8 8.98 us: flip(): return lax.ppermute(value, axis, [(i, i ^ bit) for i in range(count)])]
  transfers between devices with their start and end apart: 5 -> 16, of which waited for: 5 -> 10; matrix products, arithmetic and copies ran while one was open for 4% -> 21% of each run, Pallas kernels for 0% -> 0%
where the time goes in v1:
time: 239 us; the launch traced here: 236 us
  waiting for transfers between devices  95.6 us (40%)
  local copies, waits for them, and re-layouts  39.1 us (16%)
  blocking collectives  33.5 us (14%)
  starting transfers between devices  29.5 us (12%)
  matrix products  28.9 us (12%)
  other arithmetic  8.32 us (3%)
    ppermute x6, waiting for transfers between devices, shift(): lax.ppermute(value, axis, [(i, (i + step) % count) for i in range(count)])  38 us
    ppermute x8, waiting for transfers between devices, flip(): return lax.ppermute(value, axis, [(i, i ^ bit) for i in range(count)])  36 us
    all_gather x1, blocking collectives, ssd_block(): totals = lax.all_gather(total, 'seq')  33.5 us
    all_to_all x1, waiting for transfers between devices, ssd_block(): lax.all_to_all(scan_states(got, own), 'seq', split_axis=0, concat_axis=0,...  21.6 us
    dot_general x15, matrix products, dot(): return lax.dot_general(a, b, (dims, ((), ())), preferred_element_type=F32)  16.7 us
    dynamic_update_slice x1, local copies, waits for them, and re-layouts, per_device(): grads = lax.dynamic_update_slice_in_dim(grads, mine[:, None], here, axis=1)  9.38 us
    dynamic_update_slice x1, local copies, waits for them, and re-layouts, per_device(): lax.dynamic_update_slice_in_dim(grads, made[:, None], (here + s) % zero,...  9.38 us
    ppermute x8, starting transfers between devices, flip(): return lax.ppermute(value, axis, [(i, i ^ bit) for i in range(count)])  8.98 us
  transfers between devices with their start and end apart: 16, of which 10 were waited for; matrix products, arithmetic and copies ran while one was open for 21% of the time, Pallas kernels for 0%

profile of v1, /device:TPU:0, one launch (start us, length us, event | category | flops | bytes accessed | tf_op | source)
XLA Modules:
  0.0 236.0 jit_solution(519790630864562458)
XLA Ops:
  1.6 3.1 %collective-permute-start = (bf16[128,1024]{1,0:T(8,128)(2,1)S(1)}, bf16[128,1024]{1,0:T(8,128)(2,1)S(1)}, u32[]{:S(2)}, u32[]{:S(2)}) collective-permute-start(bf16[128,1024]{1,0:T(8,128)(2,1)S(1)} %dynamic-slice_bitcast_fusion), channel_id=1, source_target_pairs={{0,1},{1,0},{2,3},{3,2},{4,5},{5,4},{6,7},{7,6},{8,9},{9,8},{10,11... | collective-permute-start | bytes 786440 | tf_op jit(solution)/shard_map/ppermute | solution.py:12
  4.7 6.3 %collective-permute-done = bf16[128,1024]{1,0:T(8,128)(2,1)S(1)} collective-permute-done((bf16[128,1024]{1,0:T(8,128)(2,1)S(1)}, bf16[128,1024]{1,0:T(8,128)(2,1)S(1)}, u32[]{:S(2)}, u32[]{:S(2)}) %collective-permute-start) | collective-permute-done | bytes 262176 | tf_op jit(solution)/shard_map/ppermute | solution.py:12
  11.0 3.8 %fusion.147 = f32[128,2336]{0,1:T(8,128)S(1)} fusion(bf16[128,1024]{1,0:T(8,128)(2,1)S(1)} %collective-permute-done, bf16[1024,2336]{0,1:T(8,128)(2,1)} %param.7), kind=kOutput, calls=%fused_computation.279 | convolution fusion | flops 612368384 | bytes 6242304 | tf_op jit(solution)/shard_map/dot_general | solution.py:144
  14.9 1.8 collective-permute-start.1
  17.3 12.3 %collective-permute-done.1 = bf16[128,2304]{0,1:T(8,128)(2,1)S(1)} collective-permute-done((bf16[128,2304]{0,1:T(8,128)(2,1)S(1)}, bf16[128,2304]{0,1:T(8,128)(2,1)S(1)}, u32[]{:S(2)}, u32[]{:S(2)}) %collective-permute-start.1) | collective-permute-done | bytes 589856 | tf_op jit(solution)/shard_map/ppermute | solution.py:12
  29.8 3.8 %fusion.146 = (bf16[128,2336]{0,1:T(8,128)(2,1)S(1)}, f32[128,2336]{0,1:T(8,128)S(1)}) fusion(f32[128,32]{0,1:T(8,128)S(1)} %collective-permute-done.2, f32[128,2304]{0,1:T(8,128)S(1)} %convert_element_type.195, bf16[1024,2336]{0,1:T(8,128)(2,1)} %param.7, bf16[1,128,2048]{2,1,0:T(8,128)(2,1)S(1)} %copy-done.4, s32[]{:T(128)S(6)} %select_n.114), kind=kOutput, calls=%fused_computation.278 | convolution fusion | flops 613265408 | bytes 8036356 | tf_op jit(solution)/shard_map/dot_general | solution.py:142
  37.2 5.9 %all-to-all-start = ((bf16[16,2,2,64,128]{4,3,1,2,0:T(8,128)(2,1)}), bf16[16,2,2,64,128]{4,3,1,2,0:T(8,128)(2,1)S(1)}, u32[]{:S(2)}, u32[]{:S(2)}) async-start(bf16[16,2,2,64,128]{4,3,1,2,0:T(8,128)(2,1)} %copy.101), calls=%async_computation | async-start | bytes 2097152 | tf_op jit(solution)/shard_map/all_to_all | solution.py:71
  43.1 33.5 %all-gather = f32[16,1,32]{2,1,0:T(1,128)S(1)} all-gather(f32[1,1,32]{2,1,0:T(1,128)S(1)} %bitcast.497), channel_id=1, replica_groups=mesh['seq'=16,'zero'=2] {'seq'}, dimensions={0}, use_global_device_ids=true | all-gather | bytes 2176 | tf_op jit(solution)/shard_map/all_gather | solution.py:70
  79.9 5.8 %all-to-all-start.1 = ((bf16[16,2,2,64,128]{4,3,1,2,0:T(8,128)(2,1)}), bf16[16,2,2,64,128]{4,3,1,2,0:T(8,128)(2,1)S(1)}, u32[]{:S(2)}, u32[]{:S(2)}) async-start(bf16[16,2,2,64,128]{4,3,1,2,0:T(8,128)(2,1)} %pad_maximum_fusion.1), calls=%async_computation.1 | async-start | bytes 2097152 | tf_op jit(solution)/shard_map/all_to_all | solution.py:75
  87.0 21.6 %all-to-all-done.1 = bf16[16,2,2,64,128]{4,3,1,2,0:T(8,128)(2,1)S(1)} async-done(((bf16[16,2,2,64,128]{4,3,1,2,0:T(8,128)(2,1)}), bf16[16,2,2,64,128]{4,3,1,2,0:T(8,128)(2,1)S(1)}, u32[]{:S(2)}, u32[]{:S(2)}) %all-to-all-start.1) | async-done | bytes 1048608 | tf_op jit(solution)/shard_map/all_to_all | solution.py:75
  109.9 1.6 fusion.12
  117.1 1.6 collective-permute-start.3
  119.6 19.3 %collective-permute-done.5 = bf16[128,1024]{0,1:T(8,128)(2,1)S(1)} collective-permute-done((bf16[128,1024]{0,1:T(8,128)(2,1)S(1)}, bf16[128,1024]{0,1:T(8,128)(2,1)S(1)}, u32[]{:S(2)}, u32[]{:S(2)}) %collective-permute-start.5) | collective-permute-done | bytes 262176 | tf_op jit(solution)/shard_map/ppermute | solution.py:12
  139.7 1.6 convolution_convert_fusion.1
  141.3 1.5 convolution_convert_fusion
  143.3 4.1 %convolution_convert_fusion.4 = bf16[128,1024]{1,0:T(8,128)(2,1)} fusion(bf16[128,2336]{0,1:T(8,128)(2,1)S(1)} %collective-permute-done.3, bf16[1024,2336]{0,1:T(8,128)(2,1)} %param.7), kind=kOutput, calls=%fused_computation.24 | convolution fusion | flops 612499456 | bytes 5644288 | tf_op jit(solution)/shard_map/dot_general | solution.py:21
  147.4 1.5 collective-permute-start.4
  150.0 1.9 convolution_add_fusion
  152.7 2.0 collective-permute-start.7
  156.8 2.0 copy.112
  159.9 9.4 %dynamic_update_slice.6 = bf16[128,2,1024]{2,1,0:T(2,128)(2,1)} dynamic-update-slice(bf16[128,2,1024]{2,1,0:T(2,128)(2,1)} %broadcast_in_dim.22, bf16[128,1,1024]{2,1,0:T(2,128)(2,1)} %copy.106, s32[]{:T(128)} %constant.147.clone.1, s32[]{:T(128)S(6)} %select_n.121, s32[]{:T(128)} %constant.147.clone.1) | dynamic-update-slice | bytes 524292 | tf_op jit(solution)/shard_map/dynamic_update_slice | solution.py:162
  169.3 2.1 copy.107
  171.5 9.4 %dynamic_update_slice.7 = bf16[128,2,1024]{2,1,0:T(2,128)(2,1)} dynamic-update-slice(bf16[128,2,1024]{2,1,0:T(2,128)(2,1)} %dynamic_update_slice.6, bf16[128,1,1024]{2,1,0:T(2,128)(2,1)} %copy.107, s32[]{:T(128)} %constant.147.clone.1, s32[]{:T(128)S(6)} %select_n.122, s32[]{:T(128)} %constant.147.clone.1) | dynamic-update-slice | bytes 524292 | tf_op jit(solution)/shard_map/dynamic_update_slice | solution.py:165
  180.9 2.2 reshape.725
  183.1 3.3 %convolution_add_fusion.1 = f32[512,1184]{0,1:T(8,128)} fusion(bf16[256,512]{0,1:T(8,128)(2,1)} %bitcast.482, bf16[512,1184]{0,1:T(8,128)(2,1)} %collective-permute-done.10, bf16[128,2336]{0,1:T(8,128)(2,1)S(1)} %collective-permute-done.3, bf16[128,32]{0,1:T(8,128)(2,1)S(1)} %fusion.11, bf16[128,128]{0,1:T(8,128)(2,1)S(1)} %fusion.7, ...), kind=kOutput, calls=%fused_computation.1 | convolution fusion | flops 314621952 | bytes 5095424 | tf_op jit(solution)/shard_map/dot_general | solution.py:21
  186.4 3.2 %copy.111 = f32[512,1184]{1,0:T(8,128)} copy(f32[512,1184]{0,1:T(8,128)} %convolution_add_fusion.1) | data formatting | bytes 4849664 | tf_op jit(solution)/shard_map/add | solution.py:188
  191.0 2.9 %collective-permute-start.11 = (bf16[2,2,64,1184]{3,2,1,0:T(8,128)(2,1)S(1)}, bf16[2,2,64,1184]{3,2,1,0:T(8,128)(2,1)S(1)}, u32[]{:S(2)}, u32[]{:S(2)}) collective-permute-start(bf16[2,2,64,1184]{3,2,1,0:T(8,128)(2,1)S(1)} %fusion.22), channel_id=1, source_target_pairs={{0,8},{2,10},{4,12},{6,14},{8,0},{10,2},{12,4},{14,6},{16,24},{18,... | collective-permute-start | bytes 1818632 | tf_op jit(solution)/shard_map/ppermute | solution.py:17
  195.4 14.1 %collective-permute-done.11 = bf16[2,2,64,1184]{3,2,1,0:T(8,128)(2,1)S(1)} collective-permute-done((bf16[2,2,64,1184]{3,2,1,0:T(8,128)(2,1)S(1)}, bf16[2,2,64,1184]{3,2,1,0:T(8,128)(2,1)S(1)}, u32[]{:S(2)}, u32[]{:S(2)}) %collective-permute-start.11) | collective-permute-done | bytes 606240 | tf_op jit(solution)/shard_map/ppermute | solution.py:17
  209.6 1.5 collective-permute-start.12
  211.1 8.1 %collective-permute-done.8 = bf16[2,64,1152]{2,1,0:T(8,128)(2,1)S(1)} collective-permute-done((bf16[2,64,1152]{2,1,0:T(8,128)(2,1)S(1)}, bf16[2,64,1152]{2,1,0:T(8,128)(2,1)S(1)}, u32[]{:S(2)}, u32[]{:S(2)}) %collective-permute-start.8) | collective-permute-done | bytes 294944 | tf_op jit(solution)/shard_map/ppermute | solution.py:17
  220.3 9.3 %collective-permute-done.12 = bf16[2,64,1184]{2,1,0:T(8,128)(2,1)S(1)} collective-permute-done((bf16[2,64,1184]{2,1,0:T(8,128)(2,1)S(1)}, bf16[2,64,1184]{2,1,0:T(8,128)(2,1)S(1)}, u32[]{:S(2)}, u32[]{:S(2)}) %collective-permute-start.12) | collective-permute-done | bytes 303136 | tf_op jit(solution)/shard_map/ppermute | solution.py:17
  231.2 3.9 %collective-permute-done.13 = bf16[64,1184]{1,0:T(8,128)(2,1)S(1)} collective-permute-done((bf16[64,1184]{1,0:T(8,128)(2,1)S(1)}, bf16[64,1184]{1,0:T(8,128)(2,1)S(1)}, u32[]{:S(2)}, u32[]{:S(2)}) %collective-permute-start.13) | collective-permute-done | bytes 151584 | tf_op jit(solution)/shard_map/ppermute | solution.py:17
  (123 shorter events, 30.6 us)
Async XLA Ops:
  1.6 9.4 %collective-permute-start = (bf16[128,1024]{1,0:T(8,128)(2,1)S(1)}, bf16[128,1024]{1,0:T(8,128)(2,1)S(1)}, u32[]{:S(2)}, u32[]{:S(2)}) collective-permute-start(bf16[128,1024]{1,0:T(8,128)(2,1)S(1)} %dynamic-slice_bitcast_fusion), channel_id=1, source_target_pairs={{0,1},{1,0},{2,3},{3,2},{4,5},{5,4},{6,7},{7,6},{8,9},{9,8},{10,11... | collective-permute-start | bytes 786440 | tf_op jit(solution)/shard_map/ppermute | solution.py:12
  14.8 2.2 copy-start.10
  14.8 2.2 copy-start.7
  14.9 14.7 %collective-permute-start.1 = (bf16[128,2304]{0,1:T(8,128)(2,1)S(1)}, bf16[128,2304]{0,1:T(8,128)(2,1)S(1)}, u32[]{:S(2)}, u32[]{:S(2)}) collective-permute-start(bf16[128,2304]{0,1:T(8,128)(2,1)S(1)} %slice.636), channel_id=1, source_target_pairs={{0,1},{1,0},{2,3},{3,2},{4,5},{5,4},{6,7},{7,6},{8,9},{9,8},{10,11... | collective-permute-start | bytes 1769480 | tf_op jit(solution)/shard_map/ppermute | solution.py:12
  16.7 13.1 %collective-permute-start.2 = (f32[128,32]{0,1:T(8,128)S(1)}, f32[128,32]{0,1:T(8,128)S(1)}, u32[]{:S(2)}, u32[]{:S(2)}) collective-permute-start(f32[128,32]{0,1:T(8,128)S(1)} %slice.393), channel_id=1, source_target_pairs={{0,1},{1,0},{2,3},{3,2},{4,5},{5,4},{6,7},{7,6},{8,9},{9,8},{10,11... | collective-permute-start | bytes 49160 | tf_op jit(solution)/shard_map/ppermute | solution.py:12
  17.0 12.8 %copy-start.4 = (bf16[1,128,2048]{2,1,0:T(8,128)(2,1)S(1)}, bf16[1,128,2048]{2,1,0:T(8,128)(2,1)}, u32[]{:S(2)}) copy-start(bf16[1,128,2048]{2,1,0:T(8,128)(2,1)} %param.6) | copy-start | bytes 1572868
  29.7 5.0 %copy-start.9 = (f32[32]{0:T(128)S(1)}, f32[32]{0:T(128)}, u32[]{:S(2)}) copy-start(f32[32]{0:T(128)} %param.9) | copy-start | bytes 388
  33.6 1.0 copy-start.6
  37.2 39.4 %all-to-all-start = ((bf16[16,2,2,64,128]{4,3,1,2,0:T(8,128)(2,1)}), bf16[16,2,2,64,128]{4,3,1,2,0:T(8,128)(2,1)S(1)}, u32[]{:S(2)}, u32[]{:S(2)}) async-start(bf16[16,2,2,64,128]{4,3,1,2,0:T(8,128)(2,1)} %copy.101), calls=%async_computation | async-start | bytes 2097152 | tf_op jit(solution)/shard_map/all_to_all | solution.py:71
  79.9 28.7 %all-to-all-start.1 = ((bf16[16,2,2,64,128]{4,3,1,2,0:T(8,128)(2,1)}), bf16[16,2,2,64,128]{4,3,1,2,0:T(8,128)(2,1)S(1)}, u32[]{:S(2)}, u32[]{:S(2)}) async-start(bf16[16,2,2,64,128]{4,3,1,2,0:T(8,128)(2,1)} %pad_maximum_fusion.1), calls=%async_computation.1 | async-start | bytes 2097152 | tf_op jit(solution)/shard_map/all_to_all | solution.py:75
  108.7 1.2 copy-start.1
  108.7 1.2 copy-start.8
  115.8 2.9 %copy-start.5 = (bf16[1,128,2048]{2,1,0:T(8,128)(2,1)S(1)}, bf16[1,128,2048]{2,1,0:T(8,128)(2,1)}, u32[]{:S(2)}) copy-start(bf16[1,128,2048]{2,1,0:T(8,128)(2,1)} %param.6) | copy-start | bytes 1572868
  117.1 22.6 %collective-permute-start.3 = (bf16[128,2336]{0,1:T(8,128)(2,1)S(1)}, bf16[128,2336]{0,1:T(8,128)(2,1)S(1)}, u32[]{:S(2)}, u32[]{:S(2)}) collective-permute-start(bf16[128,2336]{0,1:T(8,128)(2,1)S(1)} %pad_maximum_fusion.7), channel_id=1, source_target_pairs={{0,1},{1,0},{2,3},{3,2},{4,5},{5,4},{6,7},{7,6},{8,9},{9,8},{10,11... | collective-permute-start | bytes 1794056 | tf_op jit(solution)/shard_map/ppermute | solution.py:12
  119.0 19.9 %collective-permute-start.5 = (bf16[128,1024]{0,1:T(8,128)(2,1)S(1)}, bf16[128,1024]{0,1:T(8,128)(2,1)S(1)}, u32[]{:S(2)}, u32[]{:S(2)}) collective-permute-start(bf16[128,1024]{0,1:T(8,128)(2,1)S(1)} %bitcast.492), channel_id=1, source_target_pairs={{0,1},{1,0},{2,3},{3,2},{4,5},{5,4},{6,7},{7,6},{8,9},{9,8},{10,11... | collective-permute-start | bytes 786440 | tf_op jit(solution)/shard_map/ppermute | solution.py:12
  141.3 7.7 %collective-permute-start.6 = (bf16[512,1152]{1,0:T(8,128)(2,1)}, bf16[512,1152]{1,0:T(8,128)(2,1)S(1)}, u32[]{:S(2)}, u32[]{:S(2)}) collective-permute-start(bf16[512,1152]{1,0:T(8,128)(2,1)} %convolution_convert_fusion.1), channel_id=1, source_target_pairs={{0,2},{2,0},{4,6},{6,4},{8,10},{10,8},{12,14},{14,12},{16,18},{18,... | collective-permute-start | bytes 3538952 | tf_op jit(solution)/shard_map/ppermute | solution.py:17
  142.8 7.2 %copy-start.2 = (bf16[256,8,1,64]{0,3,2,1:T(8,128)(2,1)S(1)}, bf16[256,8,1,64]{0,3,2,1:T(8,128)(2,1)}, u32[]{:S(2)}) copy-start(bf16[256,8,1,64]{0,3,2,1:T(8,128)(2,1)} %get-tuple-element.49) | copy-start | bytes 786436
  142.8 40.3 %collective-permute-start.10 = (bf16[512,1184]{0,1:T(8,128)(2,1)}, bf16[512,1184]{0,1:T(8,128)(2,1)}, u32[]{:S(2)}, u32[]{:S(2)}) collective-permute-start(bf16[512,1184]{0,1:T(8,128)(2,1)} %convolution_convert_fusion), channel_id=1, source_target_pairs={{0,2},{2,0},{4,6},{6,4},{8,10},{10,8},{12,14},{14,12},{16,18},{18,... | collective-permute-start | bytes 3637256 | tf_op jit(solution)/shard_map/ppermute | solution.py:17
  143.3 11.4 %slice-start = ((s8[4784128]{0:T(1024)(128)(4,1)}), s8[4194304]{0:T(1024)(128)(4,1)S(1)}, s32[]{:S(2)}) async-start(s8[4784128]{0:T(1024)(128)(4,1)} %bitcast.460), calls=%async_computation.2 | async-start | bytes 8388608
  147.4 21.9 %collective-permute-start.4 = (bf16[128,1024]{1,0:T(8,128)(2,1)}, bf16[128,1024]{1,0:T(8,128)(2,1)}, u32[]{:S(2)}, u32[]{:S(2)}) collective-permute-start(bf16[128,1024]{1,0:T(8,128)(2,1)} %convolution_convert_fusion.4), channel_id=1, source_target_pairs={{0,1},{1,0},{2,3},{3,2},{4,5},{5,4},{6,7},{7,6},{8,9},{9,8},{10,11... | collective-permute-start | bytes 786440 | tf_op jit(solution)/shard_map/ppermute | solution.py:12
  148.9 1.0 copy-start.3
  150.0 4.8 %slice-start.1 = ((s8[4784128]{0:T(1024)(128)(4,1)}), s8[589824]{0:T(1024)(128)(4,1)S(1)}, s32[]{:S(2)}) async-start(s8[4784128]{0:T(1024)(128)(4,1)} %bitcast.460), calls=%async_computation.3 | async-start | bytes 1179648
  152.7 41.1 %collective-permute-start.7 = (bf16[2,2,64,1152]{3,2,0,1:T(8,128)(2,1)}, bf16[2,2,64,1152]{3,2,0,1:T(8,128)(2,1)}, u32[]{:S(2)}, u32[]{:S(2)}) collective-permute-start(bf16[2,2,64,1152]{3,2,0,1:T(8,128)(2,1)} %fusion.23), channel_id=1, source_target_pairs={{0,4},{2,6},{4,0},{6,2},{8,12},{10,14},{12,8},{14,10},{16,20},{18,... | collective-permute-start | bytes 1769480 | tf_op jit(solution)/shard_map/ppermute | solution.py:17
  191.0 18.5 %copy-start = (f32[512,1184]{1,0:T(8,128)S(1)}, f32[512,1184]{1,0:T(8,128)}, u32[]{:S(2)}) copy-start(f32[512,1184]{1,0:T(8,128)} %copy.111) | copy-start | bytes 7274500
  191.0 18.5 %collective-permute-start.11 = (bf16[2,2,64,1184]{3,2,1,0:T(8,128)(2,1)S(1)}, bf16[2,2,64,1184]{3,2,1,0:T(8,128)(2,1)S(1)}, u32[]{:S(2)}, u32[]{:S(2)}) collective-permute-start(bf16[2,2,64,1184]{3,2,1,0:T(8,128)(2,1)S(1)} %fusion.22), channel_id=1, source_target_pairs={{0,8},{2,10},{4,12},{6,14},{8,0},{10,2},{12,4},{14,6},{16,24},{18,... | collective-permute-start | bytes 1818632 | tf_op jit(solution)/shard_map/ppermute | solution.py:17
  195.1 24.1 %collective-permute-start.8 = (bf16[2,64,1152]{2,1,0:T(8,128)(2,1)S(1)}, bf16[2,64,1152]{2,1,0:T(8,128)(2,1)S(1)}, u32[]{:S(2)}, u32[]{:S(2)}) collective-permute-start(bf16[2,64,1152]{2,1,0:T(8,128)(2,1)S(1)} %fusion.25), channel_id=1, source_target_pairs={{0,8},{2,10},{4,12},{6,14},{8,0},{10,2},{12,4},{14,6},{16,24},{18,... | collective-permute-start | bytes 884744 | tf_op jit(solution)/shard_map/ppermute | solution.py:17
  209.6 20.0 %collective-permute-start.12 = (bf16[2,64,1184]{2,1,0:T(8,128)(2,1)S(1)}, bf16[2,64,1184]{2,1,0:T(8,128)(2,1)S(1)}, u32[]{:S(2)}, u32[]{:S(2)}) collective-permute-start(bf16[2,64,1184]{2,1,0:T(8,128)(2,1)S(1)} %fusion.24), channel_id=1, source_target_pairs={{0,16},{2,18},{4,20},{6,22},{8,24},{10,26},{12,28},{14,30},{16,0},... | collective-permute-start | bytes 909320 | tf_op jit(solution)/shard_map/ppermute | solution.py:17
  219.3 11.9 %collective-permute-start.9 = (bf16[64,1152]{1,0:T(8,128)(2,1)S(1)}, bf16[64,1152]{1,0:T(8,128)(2,1)S(1)}, u32[]{:S(2)}, u32[]{:S(2)}) collective-permute-start(bf16[64,1152]{1,0:T(8,128)(2,1)S(1)} %fusion.34), channel_id=1, source_target_pairs={{0,16},{2,18},{4,20},{6,22},{8,24},{10,26},{12,28},{14,30},{16,0},... | collective-permute-start | bytes 442376 | tf_op jit(solution)/shard_map/ppermute | solution.py:17
  229.7 5.4 %collective-permute-start.13 = (bf16[64,1184]{1,0:T(8,128)(2,1)S(1)}, bf16[64,1184]{1,0:T(8,128)(2,1)S(1)}, u32[]{:S(2)}, u32[]{:S(2)}) collective-permute-start(bf16[64,1184]{1,0:T(8,128)(2,1)S(1)} %fusion.33), channel_id=1, source_target_pairs={{0,4},{2,6},{4,0},{6,2},{8,12},{10,14},{12,8},{14,10},{16,20},{18,... | collective-permute-start | bytes 454664 | tf_op jit(solution)/shard_map/ppermute | solution.py:17

commit v2 on v1

--- a/solution.py
+++ b/solution.py
@@ -1,10 +1,15 @@
+import functools
+
 import jax
 import jax.numpy as jnp
 from jax import lax
+from jax.experimental import pallas as pl
+from jax.experimental.pallas import tpu as pltpu
 from jax.sharding import PartitionSpec as P
 
 BF = jnp.bfloat16
 F32 = jnp.float32
+MESH = pl.DeviceIdType.MESH
 
 
 def shift(value, axis, step):
@@ -12,11 +17,6 @@
     return lax.ppermute(value, axis, [(i, (i + step) % count) for i in range(count)])
 
 
-def flip(value, axis, bit):
-    count = lax.axis_size(axis)
-    return lax.ppermute(value, axis, [(i, i ^ bit) for i in range(count)])
-
-
 def dot(a, b, dims):
     return lax.dot_general(a, b, (dims, ((), ())), preferred_element_type=F32)
 
@@ -25,17 +25,251 @@
     return jnp.einsum(spec, a, b, preferred_element_type=F32)
 
 
-def scan_states(states, totals):
-    count = states.shape[0]
-    fwd, bwd = states[:, :, 0].astype(F32), states[:, :, 1].astype(F32)
-    run, ahead = [jnp.zeros_like(fwd[0])], [jnp.zeros_like(bwd[0])]
-    for k in range(count - 1):
-        run.append(jnp.exp(totals[k])[:, None, None] * run[-1] + fwd[k])
-    for k in range(count - 1, 0, -1):
-        ahead.append(jnp.exp(totals[k])[:, None, None] * ahead[-1] + bwd[k])
-    return jnp.stack(
-        [jnp.stack(run).astype(BF), jnp.stack(ahead[::-1]).astype(BF)], axis=2
+def greet(peers):
+    barrier = pltpu.get_barrier_semaphore()
+    for peer in peers:
+        pl.semaphore_signal(barrier, inc=1, device_id={"seq": peer}, device_id_type=MESH)
+    pl.semaphore_wait(barrier, len(peers))
+
+
+def remote(src, dst, send, recv, peer):
+    return pltpu.make_async_remote_copy(
+        src_ref=src,
+        dst_ref=dst,
+        send_sem=send,
+        recv_sem=recv,
+        device_id={"seq": peer},
+        device_id_type=MESH,
     )
+
+
+def scan_kernel(
+    pair, totals, start, end, both, marks, joined, sums, got, lengths, made, back, final, wide,
+    send, recv, local
+):
+    chips, _, share = pair.shape[:3]
+    me = lax.axis_index("seq")
+    core, chip = lax.rem(me, 2), lax.div(me, 2)
+    sibling = me + 1 - 2 * core
+    places = [lax.rem(chip + d, chips) for d in range(1, chips)]
+    peers = [place * 2 + core for place in places]
+    greet([sibling] + peers)
+
+    def move(copies):
+        for copy in copies:
+            copy.start()
+        for copy in copies:
+            copy.wait()
+
+    move(
+        [
+            remote(pair.at[:, 1 - core], both.at[core], send.at[0, 0], recv.at[0, 0], sibling),
+            remote(totals.at[:, 1 - core], marks.at[core], send.at[1, 0], recv.at[1, 0], sibling),
+            pltpu.make_async_copy(pair.at[:, core], both.at[core], local.at[0]),
+            pltpu.make_async_copy(totals.at[:, core], marks.at[core], local.at[1]),
+        ]
+    )
+
+    def gain(ref, *at):
+        return jnp.exp(ref[at])
+
+    for k in range(chips):
+        sums[k] = marks[0, k] + marks[1, k]
+        for j in range(share):
+            row = pl.ds(j, 1)
+            joined[k, j, 0] = (
+                gain(marks, 1, k, row) * both[0, k, j, 0].astype(F32)
+                + both[1, k, j, 0].astype(F32)
+            ).astype(BF)
+            joined[k, j, 1] = (
+                gain(marks, 0, k, row) * both[1, k, j, 1].astype(F32)
+                + both[0, k, j, 1].astype(F32)
+            ).astype(BF)
+    copies = []
+    for d, (place, peer) in enumerate(zip(places, peers)):
+        copies.append(remote(joined.at[place], got.at[chip], send.at[2, d], recv.at[2, d], peer))
+        copies.append(remote(sums.at[place], lengths.at[chip], send.at[3, d], recv.at[3, d], peer))
+    copies.append(pltpu.make_async_copy(joined.at[chip], got.at[chip], local.at[2]))
+    copies.append(pltpu.make_async_copy(sums.at[chip], lengths.at[chip], local.at[3]))
+    move(copies)
+
+    for j in range(share):
+        row = pl.ds(j, 1)
+        run = jnp.zeros(pair.shape[4:], F32)
+        for k in range(chips):
+            made[k, j, 0] = run.astype(BF)
+            if k < chips - 1:
+                run = gain(lengths, k, row) * run + got[k, j, 0].astype(F32)
+        run = jnp.zeros(pair.shape[4:], F32)
+        for k in reversed(range(chips)):
+            made[k, j, 1] = run.astype(BF)
+            if k > 0:
+                run = gain(lengths, k, row) * run + got[k, j, 1].astype(F32)
+    copies = [
+        remote(made.at[place], back.at[chip], send.at[4, d], recv.at[4, d], peer)
+        for d, (place, peer) in enumerate(zip(places, peers))
+    ]
+    move(copies + [pltpu.make_async_copy(made.at[chip], back.at[chip], local.at[4])])
+
+    for k in range(chips):
+        for j in range(share):
+            row = pl.ds(j, 1)
+            first, last = back[k, j, 0], back[k, j, 1]
+            final[0, k, j, 0] = first
+            final[1, k, j, 1] = last
+            final[1, k, j, 0] = (
+                gain(marks, 0, k, row) * first.astype(F32) + both[0, k, j, 0].astype(F32)
+            ).astype(BF)
+            final[0, k, j, 1] = (
+                gain(marks, 1, k, row) * last.astype(F32) + both[1, k, j, 1].astype(F32)
+            ).astype(BF)
+    move(
+        [
+            remote(final.at[1 - core], wide.at[core], send.at[5, 0], recv.at[5, 0], sibling),
+            pltpu.make_async_copy(final.at[core], wide.at[core], local.at[5]),
+        ]
+    )
+    for parity in range(2):
+        start[:, parity] = wide[parity, :, :, 0]
+        end[:, parity] = wide[parity, :, :, 1]
+
+
+def scan_states(pair, totals):
+    chips, _, share, _, rows, lanes = pair.shape
+    state = jax.ShapeDtypeStruct((chips, 2, share, rows, lanes), BF)
+    half = (chips,) + pair.shape[2:]
+    short = (chips,) + totals.shape[2:]
+    return pl.pallas_call(
+        scan_kernel,
+        out_shape=(state, state),
+        in_specs=[pl.BlockSpec(memory_space=pltpu.VMEM)] * 2,
+        out_specs=[pl.BlockSpec(memory_space=pltpu.VMEM)] * 2,
+        scratch_shapes=[
+            pltpu.VMEM((2,) + half, BF),
+            pltpu.VMEM((2,) + short, F32),
+            pltpu.VMEM(half, BF),
+            pltpu.VMEM(short, F32),
+            pltpu.VMEM(half, BF),
+            pltpu.VMEM(short, F32),
+            pltpu.VMEM(half, BF),
+            pltpu.VMEM(half, BF),
+            pltpu.VMEM((2,) + half, BF),
+            pltpu.VMEM((2,) + half, BF),
+            pltpu.SemaphoreType.DMA((6, chips)),
+            pltpu.SemaphoreType.DMA((6, chips)),
+            pltpu.SemaphoreType.DMA((6,)),
+        ],
+        compiler_params=pltpu.CompilerParams(collective_id=0, has_side_effects=True),
+    )(pair, totals)
+
+
+def sum_kernel(seq, spans, tile, left, right, out, *scratch):
+    levels = (seq // 2).bit_length() - 1
+    me = lax.axis_index("seq")
+    core, place = lax.rem(me, 2), lax.div(me, 2)
+    bits = [lax.rem(lax.div(place, 1 << b), 2) for b in range(levels)]
+    sibling = me + 1 - 2 * core
+    partners = [me + (1 - 2 * bits[b]) * (2 << b) for b in range(levels)]
+    greet([sibling] + partners)
+    pieces, piece, tokens = left.shape[1:]
+    parts = len(spans)
+    up = list(range(levels))
+    orders = [up, up[1:] + up[:1]] * (parts // 2)
+    acc, away, come = (scratch[i * parts : (i + 1) * parts] for i in range(3))
+    rest = scratch[3 * parts : -2]
+    outs = [rest[h * levels : (h + 1) * levels] for h in range(parts)]
+    ins = [rest[(parts + h) * levels : (parts + h + 1) * levels] for h in range(parts)]
+    send, recv = scratch[-2:]
+
+    def multiply(side, h, target):
+        low, high = spans[h]
+        rows = left[side].reshape(pieces * piece, tokens)
+        full = (high - low) // tile
+
+        def column(first, own, wide):
+            made = jnp.dot(rows, right[:, pl.ds(first, wide)], preferred_element_type=F32)
+            target[:, :, pl.ds(own, wide)] = made.reshape(pieces, piece, wide).astype(target.dtype)
+
+        @pl.loop(0, full)
+        def _(i):
+            own = pl.multiple_of(i * tile, 128)
+            column(pl.multiple_of(low + i * tile, 128), own, tile)
+
+        if (high - low) % tile:
+            column(low + full * tile, full * tile, (high - low) % tile)
+
+    first = []
+    for h in range(parts):
+        multiply(1 - core, h, away[h])
+        copy = remote(away[h], come[h], send.at[h, levels], recv.at[h, levels], sibling)
+        copy.start()
+        first.append(copy)
+
+    def subsets(rest):
+        found = [0]
+        for b in rest:
+            found = found + [value + (1 << b) for value in found]
+        return found
+
+    def begin(h, s):
+        order = orders[h]
+        b = order[s]
+        base = sum((bits[f] * (1 << f) for f in order[:s]), 0)
+        for j, extra in enumerate(subsets(order[s + 1 :])):
+            outs[h][s][j] = acc[h][base + (1 - bits[b]) * (1 << b) + extra].astype(BF)
+        copy = remote(outs[h][s], ins[h][s], send.at[h, s], recv.at[h, s], partners[b])
+        copy.start()
+        return copy
+
+    def finish(h, s, copy):
+        copy.wait()
+        order = orders[h]
+        base = sum((bits[f] * (1 << f) for f in order[: s + 1]), 0)
+        for j, extra in enumerate(subsets(order[s + 1 :])):
+            acc[h][base + extra] += ins[h][s][j].astype(F32)
+
+    flying = []
+    for h in range(parts):
+        multiply(core, h, acc[h])
+        first[h].wait()
+
+        @pl.loop(0, pieces)
+        def _(i):
+            acc[h][i] += come[h][i].astype(F32)
+
+        flying.append(begin(h, 0))
+    for s in range(levels):
+        for h in range(parts):
+            finish(h, s, flying[h])
+            if s + 1 < levels:
+                flying[h] = begin(h, s + 1)
+    for h in range(parts):
+        out[:, spans[h][0] : spans[h][1]] = acc[h][place]
+
+
+def sum_shards(left, right):
+    pieces, piece = left.shape[1:3]
+    cols = right.shape[1]
+    seq = 2 * pieces
+    tile, parts = 256, 4
+    levels = pieces.bit_length() - 1
+    edges = [(2 * i * cols // parts + 128) // 256 * 128 for i in range(parts)] + [cols]
+    spans = list(zip(edges[:-1], edges[1:]))
+    widths = [high - low for low, high in spans]
+    scratch = [pltpu.VMEM((pieces, piece, w), F32) for w in widths]
+    scratch += [pltpu.VMEM((pieces, piece, w), BF) for w in widths] * 2
+    for _ in range(2):
+        for w in widths:
+            scratch += [pltpu.VMEM((pieces >> (s + 1), piece, w), BF) for s in range(levels)]
+    scratch += [pltpu.SemaphoreType.DMA((parts, levels + 1))] * 2
+    return pl.pallas_call(
+        functools.partial(sum_kernel, seq, spans, tile),
+        out_shape=jax.ShapeDtypeStruct((piece, cols), F32),
+        in_specs=[pl.BlockSpec(memory_space=pltpu.VMEM)] * 2,
+        out_specs=pl.BlockSpec(memory_space=pltpu.VMEM),
+        scratch_shapes=scratch,
+        compiler_params=pltpu.CompilerParams(collective_id=1, has_side_effects=True),
+    )(left, right)
 
 
 def ssd_block(proj, gy, a_log, dt_bias, d_skip):
@@ -65,16 +299,12 @@
     pair = jnp.stack([local_f.reshape(shape), local_g.reshape(shape)], axis=1).astype(BF)
 
     seq = lax.axis_size("seq")
-    mine = lax.axis_index("seq")
     share = heads // seq
-    totals = lax.all_gather(total, "seq")
-    got = lax.all_to_all(
-        pair.reshape(seq, share, 2, width, size), "seq", split_axis=0, concat_axis=0, tiled=True
-    )
-    own = lax.dynamic_slice_in_dim(totals, mine * share, share, axis=1)
-    back = lax.all_to_all(scan_states(got, own), "seq", split_axis=0, concat_axis=0, tiled=True)
-    start = back[:, :, 0].reshape(inner, size)
-    end = back[:, :, 1].reshape(inner, size)
+    marks = jnp.pad(total.reshape(seq, share), ((0, 0), (0, -share % 8)))
+    marks = jnp.broadcast_to(marks[:, :, None], marks.shape + (size,))
+    marks = marks.reshape(seq // 2, 2, -1, size)
+    start, end = scan_states(pair.reshape(seq // 2, 2, share, 2, width, size), marks)
+    start, end = start.reshape(inner, size), end.reshape(inner, size)
 
     spans = cum.T[:, :, None] - cum.T[:, None, :]
     decay = jnp.where(lower[None], jnp.exp(jnp.where(lower[None], spans, 0.0)), 0.0)
@@ -110,18 +340,6 @@
     return out.reshape(count, inner).astype(BF), gproj
 
 
-def halving(piece_sum, bits, names):
-    mine = lax.axis_index("seq")
-    for name in bits:
-        at = names.index(name)
-        bit = (mine // name) % 2
-        away = lax.dynamic_index_in_dim(piece_sum, 1 - bit, at, keepdims=False)
-        keep = lax.dynamic_index_in_dim(piece_sum, bit, at, keepdims=False)
-        piece_sum = keep + flip(away.astype(BF), "seq", name).astype(F32)
-        names = names[:at] + names[at + 1 :]
-    return piece_sum
-
-
 def per_device(tokens, w_in, a_log, dt_bias, d_skip, grad_y):
     count, width = tokens.shape[1:]
     inner = grad_y.shape[2]
@@ -131,7 +349,6 @@
     zero = lax.axis_size("zero")
     seq = lax.axis_size("seq")
     here = lax.axis_index("zero")
-    place = lax.axis_index("seq")
     owned = width // zero
     rows = tokens.reshape(count, width)
 
@@ -158,37 +375,21 @@
 
     others = [shift(gproj, "zero", s) for s in range(1, zero)]
     mine = dot(gproj, w_in, ((1,), (1,))).astype(BF)
-    grads = jnp.zeros((count, zero, owned), BF)
-    grads = lax.dynamic_update_slice_in_dim(grads, mine[:, None], here, axis=1)
+    grads = [mine]
     for s, other in zip(range(1, zero), others):
-        made = shift(dot(other, w_in, ((1,), (1,))).astype(BF), "zero", zero - s)
-        grads = lax.dynamic_update_slice_in_dim(grads, made[:, None], (here + s) % zero, axis=1)
-    grad_tokens = grads.reshape(1, count, width)
+        grads.append(shift(dot(other, w_in, ((1,), (1,))).astype(BF), "zero", zero - s))
+    blocks = []
+    for z in range(zero):
+        block = grads[0]
+        for s in range(1, zero):
+            block = jnp.where((here + s) % zero == z, grads[s], block)
+        blocks.append(block)
+    grad_tokens = jnp.concatenate(blocks, axis=1).reshape(1, count, width)
 
     left = jnp.concatenate([pieces_of(here)] + theirs, axis=0)
     right = jnp.concatenate([gproj] + others, axis=0)
-    levels = seq.bit_length() - 1
-    names = [1 << b for b in reversed(range(levels))]
-    core = place % 2
-    left = left.reshape(left.shape[0], seq // 2, 2, piece)
-
-    def partial(core_of, span):
-        chosen = lax.dynamic_index_in_dim(left, core_of, 2, keepdims=False)
-        chosen = chosen.reshape(left.shape[0], seq // 2 * piece)
-        return dot(chosen, right[:, span], ((0,), (0,)))
-
-    done = []
-    half = columns // 2 // 128 * 128
-    rest = names[:-1]
-    for span, order in (
-        (slice(0, half), rest[::-1]),
-        (slice(half, columns), rest[:-1][::-1] + rest[-1:]),
-    ):
-        swapped = flip(partial(1 - core, span).astype(BF), "seq", 1)
-        summed = partial(core, span) + swapped.astype(F32)
-        summed = summed.reshape([2] * (levels - 1) + [piece, summed.shape[1]])
-        done.append(halving(summed, order, rest))
-    grad_w = jnp.concatenate(done, axis=1)
+    left = left.reshape(left.shape[0], seq // 2, 2, piece).transpose(2, 1, 3, 0)
+    grad_w = sum_shards(left, right)
     return (y_out.reshape(1, count, inner), grad_tokens, grad_w)
 
 

time: 239 us -> 177 us (0.74); the launches traced: 236 us -> 177 us
  Pallas kernels: 0 us -> 80.9 us
  waiting for transfers between devices: 95.6 us -> 29.8 us
  blocking collectives: 33.5 us -> 0 us
  local copies, waits for them, and re-layouts: 39.1 us -> 19.7 us
  starting transfers between devices: 29.5 us -> 10.1 us
  matrix products: 28.9 us -> 26.4 us
    pallas_call x0 -> x2, Pallas kernels: none -> 80.9 us  [the longest x1 47.7 us: sum_shards(): pl.pallas_call(functools.partial(sum_kernel, seq, spans, tile), out_shape...]
    ppermute x8 -> x0, waiting for transfers between devices: 36 us -> none  [flip(): return lax.ppermute(value, axis, [(i, i ^ bit) for i in range(count)])]
    all_gather x1 -> x0, blocking collectives: 33.5 us -> none  [ssd_block(): totals = lax.all_gather(total, 'seq')]
    all_to_all x2 -> x0, waiting for transfers between devices: 21.6 us -> none  [the longest x1 21.6 us: ssd_block(): lax.all_to_all(scan_states(got, own), 'seq', split_axis=0, concat_axis=0,...]
    dynamic_update_slice x2 -> x0, local copies, waits for them, and re-layouts: 18.8 us -> none  [the longest x1 9.38 us: per_device(): grads = lax.dynamic_update_slice_in_dim(grads, mine[:, None], here, axis=1)]
    all_to_all x2 -> x0, starting transfers between devices: 11.7 us -> none  [the longest x1 5.85 us: ssd_block(): lax.all_to_all(pair.reshape(seq, share, 2, width, size), 'seq', split_axi...]
    ppermute x8 -> x0, starting transfers between devices: 8.98 us -> none  [flip(): return lax.ppermute(value, axis, [(i, i ^ bit) for i in range(count)])]
    ppermute x6, waiting for transfers between devices: 38 us -> 29.8 us  [shift(): lax.ppermute(value, axis, [(i, (i + step) % count) for i in range(count)])]
  transfers between devices with their start and end apart: 16 -> 6, of which waited for: 10 -> 4; matrix products, arithmetic and copies ran while one was open for 21% -> 25% of each run, Pallas kernels for 0% -> 46%
where the time goes in v2:
time: 177 us
  Pallas kernels  80.9 us (46%)
  waiting for transfers between devices  29.8 us (17%)
  matrix products  26.4 us (15%)
  local copies, waits for them, and re-layouts  19.7 us (11%)
  starting transfers between devices  10.1 us (6%)
  other arithmetic  8.71 us (5%)
    pallas_call x1, Pallas kernels, sum_shards(): pl.pallas_call(functools.partial(sum_kernel, seq, spans, tile), out_shape...  47.7 us
    pallas_call x1, Pallas kernels, scan_states(): pl.pallas_call(scan_kernel, out_shape=(state, state), in_specs=[pl.BlockS...  33.2 us
    ppermute x6, waiting for transfers between devices, shift(): lax.ppermute(value, axis, [(i, (i + step) % count) for i in range(count)])  29.8 us
    dot_general x11, matrix products, dot(): return lax.dot_general(a, b, (dims, ((), ())), preferred_element_type=F32)  11.5 us
    ppermute x6, starting transfers between devices, shift(): lax.ppermute(value, axis, [(i, (i + step) % count) for i in range(count)])  10.1 us
    dot_general x3, matrix products, bdot(): return jnp.einsum(spec, a, b, preferred_element_type=F32)  5.82 us
    unnamed x42, local copies, waits for them, and re-layouts  5.54 us
    dot_general x1, matrix products, per_device(): proj = jnp.dot(columns_of(here), w_in, preferred_element_type=F32)  4.08 us
  transfers between devices with their start and end apart: 6, of which 4 were waited for; matrix products, arithmetic and copies ran while one was open for 25% of the time, Pallas kernels for 46%

profile of v2, /device:TPU:0, one launch (start us, length us, event | category | flops | bytes accessed | tf_op | source)
XLA Modules:
  0.0 176.6 jit_solution(8314566155690685654)
XLA Ops:
  1.6 3.1 %collective-permute-start = (bf16[128,1024]{1,0:T(8,128)(2,1)S(1)}, bf16[128,1024]{1,0:T(8,128)(2,1)S(1)}, u32[]{:S(2)}, u32[]{:S(2)}) collective-permute-start(bf16[128,1024]{1,0:T(8,128)(2,1)S(1)} %dynamic-slice_bitcast_fusion), channel_id=1, source_target_pairs={{0,1},{1,0},{2,3},{3,2},{4,5},{5,4},{6,7},{7,6},{8,9},{9,8},{10,11... | collective-permute-start | bytes 786440 | tf_op jit(solution)/shard_map/ppermute | solution.py:17
  4.7 6.3 %collective-permute-done = bf16[128,1024]{1,0:T(8,128)(2,1)S(1)} collective-permute-done((bf16[128,1024]{1,0:T(8,128)(2,1)S(1)}, bf16[128,1024]{1,0:T(8,128)(2,1)S(1)}, u32[]{:S(2)}, u32[]{:S(2)}) %collective-permute-start) | collective-permute-done | bytes 262176 | tf_op jit(solution)/shard_map/ppermute | solution.py:17
  11.0 3.8 %fusion.49 = f32[128,2336]{0,1:T(8,128)S(1)} fusion(bf16[128,1024]{1,0:T(8,128)(2,1)S(1)} %collective-permute-done, bf16[1024,2336]{0,1:T(8,128)(2,1)} %param.7), kind=kOutput, calls=%fused_computation.93 | convolution fusion | flops 612368384 | bytes 6242304 | tf_op jit(solution)/shard_map/dot_general | solution.py:361
  14.8 1.1 copy.127
  15.9 1.7 collective-permute-start.1
  19.1 1.8 %collective-permute-start.2 = (f32[128,32]{1,0:T(8,128)S(1)}, f32[128,32]{1,0:T(8,128)S(1)}, u32[]{:S(2)}, u32[]{:S(2)}) collective-permute-start(f32[128,32]{1,0:T(8,128)S(1)} %copy.128), channel_id=1, source_target_pairs={{0,1},{1,0},{2,3},{3,2},{4,5},{5,4},{6,7},{7,6},{8,9},{9,8},{10,11... | collective-permute-start | bytes 49160 | tf_op jit(solution)/shard_map/ppermute | solution.py:17
  20.9 1.3 copy.99
  22.2 10.1 %collective-permute-done.1 = bf16[128,2304]{1,0:T(8,128)(2,1)S(1)} collective-permute-done((bf16[128,2304]{1,0:T(8,128)(2,1)}, bf16[128,2304]{1,0:T(8,128)(2,1)S(1)}, u32[]{:S(2)}, u32[]{:S(2)}) %collective-permute-start.1) | collective-permute-done | bytes 589856 | tf_op jit(solution)/shard_map/ppermute | solution.py:17
  32.4 5.2 %collective-permute-done.2 = f32[128,32]{1,0:T(8,128)S(1)} collective-permute-done((f32[128,32]{1,0:T(8,128)S(1)}, f32[128,32]{1,0:T(8,128)S(1)}, u32[]{:S(2)}, u32[]{:S(2)}) %collective-permute-start.2) | collective-permute-done | bytes 16416 | tf_op jit(solution)/shard_map/ppermute | solution.py:17
  37.6 4.1 %fusion.48 = (bf16[128,2336]{1,0:T(8,128)(2,1)S(1)}, f32[128,2336]{1,0:T(8,128)S(1)}) fusion(f32[128,32]{1,0:T(8,128)S(1)} %collective-permute-done.2, f32[128,2304]{1,0:T(8,128)S(1)} %convert_element_type.107, bf16[1024,2336]{0,1:T(8,128)(2,1)} %param.7, bf16[1,128,2048]{2,1,0:T(8,128)(2,1)S(1)} %copy-done.3, s32[]{:T(128)S(6)} %select_n.51), kind=kOutput, calls=%fused_computation.92 | convolution fusion | flops 613265408 | bytes 8085508 | tf_op jit(solution)/shard_map/dot_general | solution.py:359
  41.7 1.2 slice_convert_fusion.1
  43.8 1.1 mul.147
  44.9 1.6 copy.97
  46.4 1.1 mul.139
  47.5 2.5 %copy.95 = f32[128,2048]{1,0:T(8,128)} copy(f32[128,2048]{0,1:T(8,128)} %bitcast.111) | data formatting | bytes 2097152 | tf_op jit(solution)/shard_map/mul | solution.py:293
  50.0 1.4 multiply_convert_fusion.1
  52.5 1.1 pad_maximum_fusion.1.pair
  54.3 33.2 %shard_map.85 = (bf16[8,2,2,64,128]{4,3,2,1,0:T(8,128)(2,1)}, bf16[8,2,2,64,128]{4,3,2,1,0:T(8,128)(2,1)}) custom-call(bf16[8,2,2,2,64,128]{5,4,3,2,1,0:T(8,128)(2,1)} %pad_maximum_fusion.1.pair, f32[8,2,8,128]{3,2,1,0:T(8,128)} %broadcast_in_dim.25.totals), custom_call_target="tpu_custom_call" | custom-call | tf_op jit(solution)/shard_map/pallas_call | solution.py:142
  87.5 2.3 %fusion.28 = f32[128,32,64]{0,2,1:T(8,128)} fusion(bf16[32,64,128]{2,1,0:T(8,128)(2,1)} %bitcast.105, bf16[128,2336]{1,0:T(8,128)(2,1)S(1)} %get-tuple-element.35), kind=kOutput, calls=%fused_computation.66 | convolution fusion | flops 67108864 | bytes 1605632 | tf_op jit(solution)/shard_map/dot_general | solution.py:21
  89.8 1.5 copy.90
  91.4 3.9 %fusion.11 = (f32[128,32]{0,1:T(8,128)}, f32[128,32]{0,1:T(8,128)}, f32[32]{0:T(128)}, bf16[128,32,64]{0,2,1:T(8,128)(2,1)S(1)}, bf16[128,32,64]{0,2,1:T(8,128)(2,1)}) fusion(f32[128,2048]{0,1:T(8,128)S(1)} %copy.90, f32[128,32]{0,1:T(8,128)S(1)} %get-tuple-element.33, f32[128,32,64]{0,2,1:T(8,128)} %fusion.28, f32[128,32,64]{0,2,1:T(8,128)S(1)} %bitcast.108, ...), kind=kOutput, calls=%fused_computation.32 | convolution fusion | flops 74178528 | bytes 4882688 | tf_op jit(solution)/shard_map/hts,thp->shp/dot_general | solution.py:25
  95.3 1.1 fusion
  98.7 1.1 fusion.17
  102.0 1.2 copy.108
  104.7 1.6 collective-permute-start.3
  106.3 1.8 %copy_bitcast_fusion.left = bf16[2,8,64,256]{3,2,1,0:T(8,128)(2,1)} fusion(bf16[128,8,2,64]{0,3,2,1:T(8,128)(2,1)} %bitcast.39, bf16[128,8,2,64]{0,3,2,1:T(8,128)(2,1)S(1)} %bitcast.117), kind=kLoop, calls=%fused_computation.52 | loop fusion | flops 1048576 | bytes 1048576 | tf_op jit(solution)/shard_map/transpose | solution.py:391
  109.1 3.2 %convolution_convert_fusion.2 = bf16[128,1024]{1,0:T(8,128)(2,1)S(1)} fusion(bf16[1024,2336]{0,1:T(8,128)(2,1)} %param.7, bf16[128,32]{1,0:T(8,128)(2,1)S(1)} %fusion.10, bf16[128,128]{1,0:T(8,128)(2,1)S(1)} %fusion.9, bf16[128,128]{1,0:T(8,128)(2,1)S(1)} %fusion.8, bf16[128,2048]{1,0:T(8,128)(2,1)S(1)} %copy.108), kind=kOutput, calls=%fused_computation.20 | convolution fusion | flops 614891520 | bytes 5644288 | tf_op jit(solution)/shard_map/dot_general | solution.py:21
  112.3 8.2 %collective-permute-done.3 = bf16[128,2336]{0,1:T(8,128)(2,1)S(1)} collective-permute-done((bf16[128,2336]{0,1:T(8,128)(2,1)S(1)}, bf16[128,2336]{0,1:T(8,128)(2,1)S(1)}, u32[]{:S(2)}, u32[]{:S(2)}) %collective-permute-start.3) | collective-permute-done | bytes 598048 | tf_op jit(solution)/shard_map/ppermute | solution.py:17
  120.5 3.2 %convolution_convert_fusion.3 = bf16[128,1024]{1,0:T(8,128)(2,1)S(1)} fusion(bf16[128,2336]{0,1:T(8,128)(2,1)S(1)} %collective-permute-done.3, bf16[1024,2336]{0,1:T(8,128)(2,1)} %param.7), kind=kOutput, calls=%fused_computation.21 | convolution fusion | flops 612499456 | bytes 5644288 | tf_op jit(solution)/shard_map/dot_general | solution.py:21
  123.8 1.6 collective-permute-start.4
  125.7 1.2 pad_maximum_fusion.right
  126.8 47.7 %shard_map.86 = f32[64,2336]{1,0:T(8,128)} custom-call(bf16[2,8,64,256]{3,2,1,0:T(8,128)(2,1)} %copy_bitcast_fusion.left, bf16[256,2336]{1,0:T(8,128)(2,1)} %pad_maximum_fusion.right), custom_call_target="tpu_custom_call" | custom-call | tf_op jit(solution)/shard_map/pallas_call | solution.py:265
  (77 shorter events, 14.4 us)
Async XLA Ops:
  1.6 9.4 %collective-permute-start = (bf16[128,1024]{1,0:T(8,128)(2,1)S(1)}, bf16[128,1024]{1,0:T(8,128)(2,1)S(1)}, u32[]{:S(2)}, u32[]{:S(2)}) collective-permute-start(bf16[128,1024]{1,0:T(8,128)(2,1)S(1)} %dynamic-slice_bitcast_fusion), channel_id=1, source_target_pairs={{0,1},{1,0},{2,3},{3,2},{4,5},{5,4},{6,7},{7,6},{8,9},{9,8},{10,11... | collective-permute-start | bytes 786440 | tf_op jit(solution)/shard_map/ppermute | solution.py:17
  14.8 2.9 %copy-start.3 = (bf16[1,128,2048]{2,1,0:T(8,128)(2,1)S(1)}, bf16[1,128,2048]{2,1,0:T(8,128)(2,1)}, u32[]{:S(2)}) copy-start(bf16[1,128,2048]{2,1,0:T(8,128)(2,1)} %param.6) | copy-start | bytes 1572868
  14.8 4.2 %copy-start.15 = (f32[32]{0:T(128)S(1)}, f32[32]{0:T(128)}, u32[]{:S(2)}) copy-start(f32[32]{0:T(128)} %param.8) | copy-start | bytes 388
  15.9 16.4 %collective-permute-start.1 = (bf16[128,2304]{1,0:T(8,128)(2,1)}, bf16[128,2304]{1,0:T(8,128)(2,1)S(1)}, u32[]{:S(2)}, u32[]{:S(2)}) collective-permute-start(bf16[128,2304]{1,0:T(8,128)(2,1)} %copy.127), channel_id=1, source_target_pairs={{0,1},{1,0},{2,3},{3,2},{4,5},{5,4},{6,7},{7,6},{8,9},{9,8},{10,11... | collective-permute-start | bytes 1769480 | tf_op jit(solution)/shard_map/ppermute | solution.py:17
  18.7 87.6 %collective-permute-start.5 = (bf16[128,1024]{0,1:T(8,128)(2,1)}, bf16[128,1024]{0,1:T(8,128)(2,1)}, u32[]{:S(2)}, u32[]{:S(2)}) collective-permute-start(bf16[128,1024]{0,1:T(8,128)(2,1)} %bitcast.38), channel_id=1, source_target_pairs={{0,1},{1,0},{2,3},{3,2},{4,5},{5,4},{6,7},{7,6},{8,9},{9,8},{10,11... | collective-permute-start | bytes 786440 | tf_op jit(solution)/shard_map/ppermute | solution.py:17
  19.0 24.2 %copy-start.12 = (f32[32]{0:T(128)}, f32[32]{0:T(128)S(1)}, u32[]{:S(2)}) copy-start(f32[32]{0:T(128)S(1)} %exponential_negate_fusion) | copy-start | bytes 388
  19.1 18.5 %collective-permute-start.2 = (f32[128,32]{1,0:T(8,128)S(1)}, f32[128,32]{1,0:T(8,128)S(1)}, u32[]{:S(2)}, u32[]{:S(2)}) collective-permute-start(f32[128,32]{1,0:T(8,128)S(1)} %copy.128), channel_id=1, source_target_pairs={{0,1},{1,0},{2,3},{3,2},{4,5},{5,4},{6,7},{7,6},{8,9},{9,8},{10,11... | collective-permute-start | bytes 49160 | tf_op jit(solution)/shard_map/ppermute | solution.py:17
  32.4 10.7 %copy-start.10 = (f32[32]{0:T(128)S(1)}, f32[32]{0:T(128)}, u32[]{:S(2)}) copy-start(f32[32]{0:T(128)} %param.9) | copy-start | bytes 388
  41.7 1.4 copy-start.4
  43.7 3.8 %copy-start.6 = (f32[1,32]{1,0:T(1,128)}, f32[1,32]{1,0:T(1,128)S(1)}, u32[]{:S(2)}) copy-start(f32[1,32]{1,0:T(1,128)S(1)} %copy.129) | copy-start | bytes 388
  87.5 3.9 %copy-start.8 = (f32[32]{0:T(128)S(1)}, f32[32]{0:T(128)}, u32[]{:S(2)}) copy-start(f32[32]{0:T(128)} %param.10) | copy-start | bytes 388
  96.4 1.0 copy-start.1
  96.4 1.3 copy-start
  97.2 1.5 copy-start.9
  99.8 3.4 %copy-start.7 = (f32[1,32]{1,0:T(1,128)S(1)}, f32[1,32]{1,0:T(1,128)}, u32[]{:S(2)}) copy-start(f32[1,32]{1,0:T(1,128)} %copy-done.6) | copy-start | bytes 388
  99.8 3.4 %copy-start.14 = (f32[32]{0:T(128)S(1)}, f32[32]{0:T(128)}, u32[]{:S(2)}) copy-start(f32[32]{0:T(128)} %get-tuple-element.21) | copy-start | bytes 388
  99.8 3.5 %copy-start.5 = (f32[128,32]{0,1:T(8,128)S(1)}, f32[128,32]{0,1:T(8,128)}, u32[]{:S(2)}) copy-start(f32[128,32]{0,1:T(8,128)} %get-tuple-element.24) | copy-start | bytes 49156
  99.8 3.5 %copy-start.11 = (f32[32]{0:T(128)S(1)}, f32[32]{0:T(128)}, u32[]{:S(2)}) copy-start(f32[32]{0:T(128)} %param.9) | copy-start | bytes 388
  99.8 3.5 %copy-start.13 = (f32[32]{0:T(128)S(1)}, f32[32]{0:T(128)}, u32[]{:S(2)}) copy-start(f32[32]{0:T(128)} %copy-done.12) | copy-start | bytes 388
  99.8 3.5 %copy-start.16 = (f32[128,32]{0,1:T(8,128)S(1)}, f32[128,32]{0,1:T(8,128)}, u32[]{:S(2)}) copy-start(f32[128,32]{0,1:T(8,128)} %get-tuple-element.19) | copy-start | bytes 49156
  104.7 15.8 %collective-permute-start.3 = (bf16[128,2336]{0,1:T(8,128)(2,1)S(1)}, bf16[128,2336]{0,1:T(8,128)(2,1)S(1)}, u32[]{:S(2)}, u32[]{:S(2)}) collective-permute-start(bf16[128,2336]{0,1:T(8,128)(2,1)S(1)} %copy.109), channel_id=1, source_target_pairs={{0,1},{1,0},{2,3},{3,2},{4,5},{5,4},{6,7},{7,6},{8,9},{9,8},{10,11... | collective-permute-start | bytes 1794056 | tf_op jit(solution)/shard_map/ppermute | solution.py:17
  123.8 50.8 %collective-permute-start.4 = (bf16[128,1024]{1,0:T(8,128)(2,1)S(1)}, bf16[128,1024]{1,0:T(8,128)(2,1)S(1)}, u32[]{:S(2)}, u32[]{:S(2)}) collective-permute-start(bf16[128,1024]{1,0:T(8,128)(2,1)S(1)} %convolution_convert_fusion.3), channel_id=1, source_target_pairs={{0,1},{1,0},{2,3},{3,2},{4,5},{5,4},{6,7},{7,6},{8,9},{9,8},{10,11... | collective-permute-start | bytes 786440 | tf_op jit(solution)/shard_map/ppermute | solution.py:17
  174.5 1.2 copy-start.2
